TPU v7x, 512 devices: a whole 4x8x8 slice. The times are simulated.
512 devices in a mesh: probe: 4 (over x), seq: 128 (over y, z, core).
Axes of the slice: x: 4, y: 8, z: 8, core: 2. Of those that a mesh axis runs over, the one named last changes fastest.
Arguments:
- probe_bits: int32 [4, 128, 16384], P('probe', 'seq'), may hold values from 0 to 1
- noise_var: float32 [128, 16384], P('seq'), may hold values from 0.2 to 12
- kernel_spectrum: float32 [16384, 128], P('seq'), may hold values from 0.05 to 4, as said below
- symbol: float32 [16384, 128], P('seq'), may hold values from 0.3 to 3, as said below
- grad_prev: float32 [16384, 128], P('seq', 'probe'), may hold values from -6 to 6
Outputs:
- residual: float32 [4, 128, 16384], P('probe', 'seq')
- grad_total: float32 [16384, 128], P('seq', 'probe')
Inputs may be any that keep to these rules, and one draw needn't show every extreme that they name: kernel_spectrum at frequency k equals kernel_spectrum at frequency (2097152 - k) mod 2097152. symbol at frequency k equals symbol at frequency (2097152 - k) mod 2097152.
All inputs are finite; a program needn't handle non-finite values.
Results may differ from a plain program's by a relative error of at most 0.00017.
Values sent between devices are 32-bit elements; how exact they have to be, the bound alone decides.
A program may use at most 64 MiB of HBM per device.

v0:
```python
import math
import jax
import jax.numpy as jnp
from jax import lax
from jax.sharding import PartitionSpec as P

highest = lax.Precision.HIGHEST
minor_width = 128


def dft_table(height, breadth, modulus, orient):
    left_index = jnp.arange(height, dtype=jnp.int32)[:, None]
    right_index = jnp.arange(breadth, dtype=jnp.int32)[None, :]
    phases = (
        orient * 2.0 * math.pi / modulus * (left_index * right_index % modulus).astype(jnp.float32)
    )
    return (jnp.cos(phases), jnp.sin(phases))


def complex_product(pattern, real_part, imaginary, cosine_table, sine_table):
    real_cos = jnp.einsum(pattern, real_part, cosine_table, precision=highest)
    real_sin = jnp.einsum(pattern, real_part, sine_table, precision=highest)
    if imaginary is None:
        return (real_cos, real_sin)
    imag_cos = jnp.einsum(pattern, imaginary, cosine_table, precision=highest)
    imag_sin = jnp.einsum(pattern, imaginary, sine_table, precision=highest)
    return (real_cos - imag_sin, real_sin + imag_cos)


def rotate(real_part, imaginary, cosine_table, sine_table):
    return (
        real_part * cosine_table - imaginary * sine_table,
        real_part * sine_table + imaginary * cosine_table,
    )


def forward_rows(series):
    major_len = series.shape[-2]
    length = major_len * minor_width
    cosine_table, sine_table = dft_table(major_len, major_len, major_len, -1.0)
    section_real, section_imag = complex_product(
        "...mi,mk->...ik", series, None, cosine_table, sine_table
    )
    turn_cos, turn_sin = dft_table(minor_width, major_len, length, -1.0)
    twisted_real, twisted_imag = rotate(section_real, section_imag, turn_cos, turn_sin)
    cosine_table, sine_table = dft_table(minor_width, minor_width, minor_width, -1.0)
    return complex_product("...ik,ij->...jk", twisted_real, twisted_imag, cosine_table, sine_table)


def inverse_rows(real_part, imaginary):
    major_len = real_part.shape[-1]
    length = major_len * minor_width
    cosine_table, sine_table = dft_table(minor_width, minor_width, minor_width, 1.0)
    section_real, section_imag = complex_product(
        "...jk,ji->...ik", real_part, imaginary, cosine_table, sine_table
    )
    turn_cos, turn_sin = dft_table(minor_width, major_len, length, 1.0)
    twisted_real, twisted_imag = rotate(section_real, section_imag, turn_cos, turn_sin)
    cosine_table, sine_table = dft_table(major_len, major_len, major_len, 1.0)
    final_real, unused = complex_product(
        "...ik,km->...mi", twisted_real, twisted_imag, cosine_table, sine_table
    )
    return final_real


def global_twiddle(local_rows, major_len, samples, orient):
    row_index = lax.axis_index("seq") * local_rows + jnp.arange(local_rows, dtype=jnp.int32)
    column_index = (
        jnp.arange(minor_width, dtype=jnp.int32)[:, None] * major_len
        + jnp.arange(major_len, dtype=jnp.int32)[None, :]
    )
    phases = (
        orient
        * 2.0
        * math.pi
        / samples
        * (row_index[:, None, None] * column_index[None, :, :] % samples).astype(jnp.float32)
    )
    return (jnp.cos(phases), jnp.sin(phases))


def forward_spectrum(series):
    local_rows = series.shape[1]
    major_len = series.shape[2]
    devices = lax.axis_size("seq")
    all_rows = local_rows * devices
    samples = all_rows * major_len * minor_width
    real_part, imaginary = forward_rows(series)
    turn_cos, turn_sin = global_twiddle(local_rows, major_len, samples, -1.0)
    turned_real, turned_imag = rotate(real_part, imaginary, turn_cos, turn_sin)
    arrived = lax.all_to_all(
        jnp.stack([turned_real, turned_imag]), "seq", split_axis=3, concat_axis=2, tiled=True
    )
    block = minor_width // devices * major_len
    arrived = arrived.reshape(arrived.shape[0], arrived.shape[1], all_rows, block)
    cosine_table, sine_table = dft_table(all_rows, all_rows, all_rows, -1.0)
    return complex_product("zrb,ra->zba", arrived[0], arrived[1], cosine_table, sine_table)


def inverse_field(spectrum_real, spectrum_imag):
    all_rows = spectrum_real.shape[2]
    block = spectrum_real.shape[1]
    devices = lax.axis_size("seq")
    major_len = block * devices // minor_width
    cosine_table, sine_table = dft_table(all_rows, all_rows, all_rows, 1.0)
    back_real, back_imag = complex_product(
        "zba,ar->zrb", spectrum_real, spectrum_imag, cosine_table, sine_table
    )
    stacked = jnp.stack([back_real, back_imag])
    stacked = stacked.reshape(
        stacked.shape[0], stacked.shape[1], all_rows, minor_width // devices, major_len
    )
    arrived = lax.all_to_all(stacked, "seq", split_axis=2, concat_axis=3, tiled=True)
    local_rows = arrived.shape[2]
    samples = all_rows * major_len * minor_width
    turn_cos, turn_sin = global_twiddle(local_rows, major_len, samples, 1.0)
    turned_real, turned_imag = rotate(arrived[0], arrived[1], turn_cos, turn_sin)
    return inverse_rows(turned_real, turned_imag) / samples


def shards(probe_bits, noise_var, kernel_spectrum, symbol, grad_prev):
    field_shape = (
        probe_bits.shape[0],
        probe_bits.shape[1],
        probe_bits.shape[2] // minor_width,
        minor_width,
    )
    sign_field = (2 * probe_bits - 1).astype(jnp.float32).reshape(field_shape)
    noise_field = noise_var.reshape(field_shape[1:])
    samples = kernel_spectrum.shape[1] * noise_var.shape[1]
    base_real, base_imag = forward_spectrum(sign_field)
    scaled_real = base_real / symbol
    scaled_imag = base_imag / symbol
    precond = inverse_field(scaled_real, scaled_imag)
    again_real, again_imag = forward_spectrum(precond)
    circulant = inverse_field(kernel_spectrum * again_real, kernel_spectrum * again_imag)
    kernel_image = circulant + noise_field * precond
    numerator, curvature = lax.psum(
        (jnp.sum(sign_field * precond), jnp.sum(precond * kernel_image)), "seq"
    )
    step_size = numerator / curvature
    residual = sign_field - step_size * kernel_image
    cross_term = lax.psum(jnp.sum(residual * kernel_image), "seq")
    weight = -2.0 * cross_term
    resid_real, resid_imag = forward_spectrum(residual)
    applied = (
        inverse_field(kernel_spectrum * resid_real, kernel_spectrum * resid_imag)
        + noise_field * residual
    )
    adjoint = (
        weight / curvature * sign_field
        - 2.0 * weight * step_size / curvature * kernel_image
        - 2.0 * step_size * applied
    )
    adjoint_real, adjoint_imag = forward_spectrum(adjoint)
    local_grad = -(adjoint_real[0] * base_real[0] + adjoint_imag[0] * base_imag[0]) / (
        samples * symbol * symbol
    )
    probes = lax.axis_size("probe")
    summed = lax.psum(local_grad, "probe")
    share_width = summed.shape[1] // probes
    own_share = lax.dynamic_slice_in_dim(
        summed, lax.axis_index("probe") * share_width, share_width, 1
    )
    grad_total = grad_prev + own_share / probes
    return (residual.reshape(probe_bits.shape), grad_total)


def solution(mesh):
    placed = (
        P("probe", "seq", None),
        P("seq", None),
        P("seq", None),
        P("seq", None),
        P("seq", "probe"),
    )
    return jax.shard_map(
        shards,
        mesh=mesh,
        in_specs=placed,
        out_specs=(P("probe", "seq", None), P("seq", "probe")),
        check_vma=False,
    )
```

profile of v0, /device:TPU:8, one launch (start us, length us, event | category | flops | bytes accessed | tf_op | source)
XLA Modules:
  0.0 741.7 jit_solution(7742233880407343323)
XLA Ops:
  7.2 0.9 add_convert_fusion
  9.0 0.7 fusion.76
  9.7 0.7 fusion.64
  10.5 0.7 convolution_add_fusion.13
  11.2 0.9 subtract_bitcast_fusion.3
  12.2 29.0 %all_to_all.28 = f32[2,1,1,128,128]{4,2,1,0,3:T(1,128)S(1)} all-to-all(f32[2,1,1,128,128]{4,2,1,0,3:T(1,128)S(1)} %copy.13), channel_id=1, replica_groups=mesh['probe'=4,'seq'=128] {'seq'}, dimensions={3} | all-to-all | bytes 262144 | tf_op jit(solution)/shard_map/all_to_all | solution.py:91
  43.1 0.5 fusion.83
  43.7 0.5 fusion.89
  44.6 0.5 fusion.18
  45.2 0.5 fusion.17
  45.9 18.2 %all_to_all.29 = f32[2,1,128,1,128]{4,3,1,0,2:T(1,128)S(1)} all-to-all(f32[2,1,128,1,128]{4,3,1,0,2:T(1,128)S(1)} %copy.14), channel_id=1, replica_groups=mesh['probe'=4,'seq'=128] {'seq'}, dimensions={2} | all-to-all | bytes 262144 | tf_op jit(solution)/shard_map/all_to_all | solution.py:113
  64.1 0.7 fusion.82
  64.9 0.7 fusion.88
  65.6 0.7 convolution_subtract_fusion.13
  66.4 0.7 convolution_add_fusion.10
  67.1 0.8 fusion.43
  67.9 0.8 fusion.16
  69.6 0.7 fusion.61
  70.3 0.7 fusion.73
  71.0 0.7 convolution_add_fusion.9
  71.7 0.9 subtract_bitcast_fusion.2
  72.8 18.1 %all_to_all.30 = f32[2,1,1,128,128]{4,2,1,0,3:T(1,128)S(1)} all-to-all(f32[2,1,1,128,128]{4,2,1,0,3:T(1,128)S(1)} %copy.17), channel_id=1, replica_groups=mesh['probe'=4,'seq'=128] {'seq'}, dimensions={3} | all-to-all | bytes 262144 | tf_op jit(solution)/shard_map/all_to_all | solution.py:91
  92.7 0.5 fusion.81
  93.3 0.5 fusion.87
  94.3 0.5 fusion.13
  94.8 0.5 fusion.12
  95.5 17.8 %all_to_all.31 = f32[2,1,128,1,128]{4,3,1,0,2:T(1,128)S(1)} all-to-all(f32[2,1,128,1,128]{4,3,1,0,2:T(1,128)S(1)} %copy.18), channel_id=1, replica_groups=mesh['probe'=4,'seq'=128] {'seq'}, dimensions={2} | all-to-all | bytes 262144 | tf_op jit(solution)/shard_map/all_to_all | solution.py:113
  113.4 0.7 fusion.80
  114.1 0.7 fusion.86
  114.9 0.7 convolution_subtract_fusion.8
  115.6 0.7 convolution_add_fusion.6
  116.4 0.8 fusion.36
  117.2 1.4 multiply_reduce_fusion.1
  118.6 213.3 %all-reduce = (f32[]{:T(128)}, f32[]{:T(128)}) all-reduce(f32[]{:T(128)} %get-tuple-element.7, f32[]{:T(128)} %get-tuple-element.6), channel_id=1, replica_groups=mesh['probe'=4,'seq'=128] {'seq'}, use_global_device_ids=true, to_apply=%region_1.2 | all-reduce | flops 2 | bytes 16 | tf_op jit(solution)/shard_map/psum | solution.py:138
  333.2 0.7 multiply_reduce_fusion
  334.8 0.7 fusion.58
  335.5 0.7 fusion.70
  336.3 0.7 convolution_add_fusion.5
  337.0 0.9 subtract_bitcast_fusion.1
  338.0 53.9 %all_to_all.32 = f32[2,1,1,128,128]{4,2,1,0,3:T(1,128)S(1)} all-to-all(f32[2,1,1,128,128]{4,2,1,0,3:T(1,128)S(1)} %copy.21), channel_id=1, replica_groups=mesh['probe'=4,'seq'=128] {'seq'}, dimensions={3} | all-to-all | bytes 262144 | tf_op jit(solution)/shard_map/all_to_all | solution.py:91
  392.9 0.5 fusion.9
  393.4 0.5 fusion.79
  393.9 0.5 fusion.85
  394.9 0.5 fusion.7
  395.4 0.5 fusion.6
  396.0 0.8 copy.22
  396.8 6.6 all-to-all-start.5
  403.4 217.7 %psum.30 = f32[]{:T(128)} all-reduce(f32[]{:T(128)} %get-tuple-element.10), channel_id=1, replica_groups=mesh['probe'=4,'seq'=128] {'seq'}, use_global_device_ids=true, to_apply=%region_5.6 | all-reduce | flops 1 | bytes 8 | tf_op jit(solution)/shard_map/psum | solution.py:143
  623.9 0.7 fusion.78
  624.7 0.7 fusion.84
  625.4 0.7 convolution_subtract_fusion.3
  626.2 0.7 convolution_add_fusion.2
  626.9 0.8 fusion.29
  627.7 0.8 fusion.20
  629.4 0.7 fusion.55
  630.1 0.7 fusion.67
  630.8 0.7 convolution_add_fusion.1
  631.5 0.9 subtract_bitcast_fusion
  632.6 53.0 %all_to_all.33 = f32[2,1,1,128,128]{4,2,1,0,3:T(1,128)S(1)} all-to-all(f32[2,1,1,128,128]{4,2,1,0,3:T(1,128)S(1)} %copy.25), channel_id=1, replica_groups=mesh['probe'=4,'seq'=128] {'seq'}, dimensions={3} | all-to-all | bytes 262144 | tf_op jit(solution)/shard_map/all_to_all | solution.py:91
  687.1 1.1 fusion.21
  688.2 0.7 copy-done.1
  689.0 44.0 %all-reduce.3.cloned.1.call-done = f32[128,128]{1,0:T(8,128)} async-done(((f32[128,128]{1,0:T(8,128)}), f32[128,128]{1,0:T(8,128)}) %all-reduce.3.cloned.1.call-update) | async-done | bytes 65552 | tf_op jit(solution)/shard_map/psum | solution.py:160
  733.0 0.9 multiply_add_fusion
  734.0 0.7 copy.31
  (56 shorter events, 12.6 us)
Async XLA Ops:
  42.3 0.8 copy-start.4
  91.4 0.8 copy-start.2
  116.4 0.8 copy-start.3
  333.9 293.8 %copy-start = (f32[128,128]{1,0:T(8,128)}, f32[128,128]{1,0:T(8,128)S(1)}, u32[]{:S(2)}) copy-start(f32[128,128]{1,0:T(8,128)S(1)} %get-tuple-element.11) | copy-start | bytes 196612
  396.8 227.0 %all-to-all-start.5 = ((f32[2,1,128,1,128]{4,3,1,0,2:T(1,128)}), f32[2,1,128,1,128]{4,3,1,0,2:T(1,128)S(1)}, u32[]{:S(2)}, u32[]{:S(2)}) async-start(f32[2,1,128,1,128]{4,3,1,0,2:T(1,128)} %copy.22), calls=%async_computation.5 | async-start | bytes 262144 | tf_op jit(solution)/shard_map/all_to_all | solution.py:113
  403.4 329.7 %all-reduce.3.cloned.1.call-start = ((), (), s32[]{:S(2)}) async-start(), calls=%async_computation.7 | async-start | bytes 131072 | tf_op jit(solution)/shard_map/psum | solution.py:160
  688.2 0.7 copy-start.1
Sparse Core Ops, SparseCore 0:
  688.3 44.6 all-reduce.2
where the time goes:
time: 750 us; the launch traced here: 742 us
  blocking collectives  621 us (83%)
  waiting for transfers between devices  44.1 us (6%)
  matrix products  43.9 us (6%)
  between operations  18.9 us (3%)
    psum x1, blocking collectives, shards(): cross_term = lax.psum(jnp.sum(residual * kernel_image), 'seq')  218 us
    psum x1, blocking collectives, shards(): lax.psum((jnp.sum(sign_field * precond), jnp.sum(precond * kernel_image))...  213 us
    all_to_all x4, blocking collectives, forward_spectrum(): lax.all_to_all(jnp.stack([turned_real, turned_imag]), 'seq', split_axis=3...  154 us
    psum x1, waiting for transfers between devices, shards(): summed = lax.psum(local_grad, 'probe')  44 us
    all_to_all x2, blocking collectives, inverse_field(): lax.all_to_all(stacked, 'seq', split_axis=2, concat_axis=3, tiled=True)  36 us
  transfers between devices with their start and end apart: 2, of which 1 were waited for; matrix products, arithmetic and copies ran while one was open for 0% of the time, Pallas kernels for 0%

commit v1 on v0

--- a/solution.py
+++ b/solution.py
@@ -6,6 +6,15 @@
 
 highest = lax.Precision.HIGHEST
 minor_width = 128
+
+
+def added_up(x, mesh_axis):
+    size = lax.axis_size(mesh_axis)
+    summed, far = (x, 1)
+    while far < size:
+        summed = summed + lax.ppermute(summed, mesh_axis, [(i, i ^ far) for i in range(size)])
+        far = 2 * far
+    return summed
 
 
 def dft_table(height, breadth, modulus, orient):
@@ -157,7 +166,7 @@
         samples * symbol * symbol
     )
     probes = lax.axis_size("probe")
-    summed = lax.psum(local_grad, "probe")
+    summed = added_up(local_grad, "probe")
     share_width = summed.shape[1] // probes
     own_share = lax.dynamic_slice_in_dim(
         summed, lax.axis_index("probe") * share_width, share_width, 1

time: 750 us -> 707 us (0.943)
  the two profiles are of different devices: /device:TPU:8 before, /device:TPU:4 now
where the time goes in v1:
time: 707 us; the launch traced here: 698 us
  blocking collectives  593 us (84%)
  matrix products  43.7 us (6%)
  starting transfers between devices  29.6 us (4%)
  waiting for transfers between devices  20.5 us (3%)
    psum x1, blocking collectives, shards(): cross_term = lax.psum(jnp.sum(residual * kernel_image), 'seq')  253 us
    psum x1, blocking collectives, shards(): lax.psum((jnp.sum(sign_field * precond), jnp.sum(precond * kernel_image))...  248 us
    all_to_all x3, blocking collectives, forward_spectrum(): lax.all_to_all(jnp.stack([turned_real, turned_imag]), 'seq', split_axis=3...  55.9 us
    all_to_all x2, blocking collectives, inverse_field(): lax.all_to_all(stacked, 'seq', split_axis=2, concat_axis=3, tiled=True)  35.9 us
    all_to_all x1, starting transfers between devices, forward_spectrum(): lax.all_to_all(jnp.stack([turned_real, turned_imag]), 'seq', split_axis=3...  17.9 us
  transfers between devices with their start and end apart: 4, of which 3 were waited for; matrix products, arithmetic and copies ran while one was open for 0% of the time, Pallas kernels for 0%

profile of v1, /device:TPU:4, one launch (start us, length us, event | category | flops | bytes accessed | tf_op | source)
XLA Modules:
  0.0 697.7 jit_solution(15943721043480661680)
XLA Ops:
  0.6 0.9 add_convert_fusion
  2.5 0.7 fusion.76
  3.2 0.7 fusion.64
  3.9 0.7 convolution_add_fusion.13
  4.6 0.9 subtract_bitcast_fusion.3
  5.5 0.8 copy.11
  6.3 17.9 %all-to-all-start = ((f32[2,1,1,128,128]{4,2,1,0,3:T(1,128)}), f32[2,1,1,128,128]{4,2,1,0,3:T(1,128)S(1)}, u32[]{:S(2)}, u32[]{:S(2)}) async-start(f32[2,1,1,128,128]{4,2,1,0,3:T(1,128)} %copy.11), calls=%async_computation | async-start | bytes 262144 | tf_op jit(solution)/shard_map/all_to_all | solution.py:100
  24.4 12.2 %all-to-all-done = f32[2,1,1,128,128]{4,2,1,0,3:T(1,128)S(1)} async-done(((f32[2,1,1,128,128]{4,2,1,0,3:T(1,128)}), f32[2,1,1,128,128]{4,2,1,0,3:T(1,128)S(1)}, u32[]{:S(2)}, u32[]{:S(2)}) %all-to-all-start) | async-done | bytes 131104 | tf_op jit(solution)/shard_map/all_to_all | solution.py:100
  36.7 0.5 fusion.75
  37.8 0.5 convolution_subtract_fusion.15
  38.3 0.5 fusion.89
  39.3 0.5 convolution_add_fusion.12
  40.4 0.5 fusion.18
  41.1 18.1 %all_to_all.28 = f32[2,1,128,1,128]{4,3,1,0,2:T(1,128)S(1)} all-to-all(f32[2,1,128,1,128]{4,3,1,0,2:T(1,128)S(1)} %copy.14), channel_id=1, replica_groups=mesh['probe'=4,'seq'=128] {'seq'}, dimensions={2} | all-to-all | bytes 262144 | tf_op jit(solution)/shard_map/all_to_all | solution.py:122
  59.2 0.7 fusion.88
  60.0 0.7 fusion.82
  60.7 0.7 convolution_add_fusion.10
  61.5 0.7 convolution_subtract_fusion.13
  62.2 0.8 fusion.43
  63.0 0.8 fusion.16
  64.7 0.7 fusion.73
  65.4 0.7 fusion.61
  66.1 0.7 convolution_add_fusion.9
  66.8 0.9 subtract_bitcast_fusion.2
  67.9 18.1 %all_to_all.29 = f32[2,1,1,128,128]{4,2,1,0,3:T(1,128)S(1)} all-to-all(f32[2,1,1,128,128]{4,2,1,0,3:T(1,128)S(1)} %copy.17), channel_id=1, replica_groups=mesh['probe'=4,'seq'=128] {'seq'}, dimensions={3} | all-to-all | bytes 262144 | tf_op jit(solution)/shard_map/all_to_all | solution.py:100
  89.4 0.5 fusion.13
  90.6 17.8 %all_to_all.30 = f32[2,1,128,1,128]{4,3,1,0,2:T(1,128)S(1)} all-to-all(f32[2,1,128,1,128]{4,3,1,0,2:T(1,128)S(1)} %copy.18), channel_id=1, replica_groups=mesh['probe'=4,'seq'=128] {'seq'}, dimensions={2} | all-to-all | bytes 262144 | tf_op jit(solution)/shard_map/all_to_all | solution.py:122
  108.5 0.7 fusion.86
  109.3 0.7 fusion.80
  110.0 0.7 convolution_add_fusion.6
  110.7 0.7 convolution_subtract_fusion.8
  111.5 0.8 fusion.36
  112.3 1.4 multiply_reduce_fusion.1
  113.7 248.0 %all-reduce = (f32[]{:T(128)}, f32[]{:T(128)}) all-reduce(f32[]{:T(128)} %get-tuple-element.3, f32[]{:T(128)} %get-tuple-element.2), channel_id=1, replica_groups=mesh['probe'=4,'seq'=128] {'seq'}, use_global_device_ids=true, to_apply=%region_1.2 | all-reduce | flops 2 | bytes 16 | tf_op jit(solution)/shard_map/psum | solution.py:147
  363.0 0.7 multiply_reduce_fusion
  364.6 0.7 fusion.70
  365.3 0.7 fusion.58
  366.1 0.7 convolution_add_fusion.5
  366.8 0.9 subtract_bitcast_fusion.1
  367.8 19.3 %all_to_all.31 = f32[2,1,1,128,128]{4,2,1,0,3:T(1,128)S(1)} all-to-all(f32[2,1,1,128,128]{4,2,1,0,3:T(1,128)S(1)} %copy.21), channel_id=1, replica_groups=mesh['probe'=4,'seq'=128] {'seq'}, dimensions={3} | all-to-all | bytes 262144 | tf_op jit(solution)/shard_map/all_to_all | solution.py:100
  388.6 0.5 fusion.85
  390.1 0.5 fusion.7
  391.2 0.8 copy.22
  392.0 6.1 all-to-all-start.5
  398.1 252.8 %psum.23 = f32[]{:T(128)} all-reduce(f32[]{:T(128)} %get-tuple-element.6), channel_id=1, replica_groups=mesh['probe'=4,'seq'=128] {'seq'}, use_global_device_ids=true, to_apply=%region_5.6 | all-reduce | flops 1 | bytes 8 | tf_op jit(solution)/shard_map/psum | solution.py:152
  653.8 0.7 fusion.84
  654.5 0.7 fusion.78
  655.3 0.7 convolution_add_fusion.2
  656.0 0.7 convolution_subtract_fusion.3
  656.8 0.8 fusion.29
  657.5 0.8 fusion.20
  659.2 0.7 fusion.67
  659.9 0.7 fusion.55
  660.7 0.7 convolution_add_fusion.1
  661.4 0.9 subtract_bitcast_fusion
  662.4 18.5 %all_to_all.32 = f32[2,1,1,128,128]{4,2,1,0,3:T(1,128)S(1)} all-to-all(f32[2,1,1,128,128]{4,2,1,0,3:T(1,128)S(1)} %copy.25), channel_id=1, replica_groups=mesh['probe'=4,'seq'=128] {'seq'}, dimensions={3} | all-to-all | bytes 262144 | tf_op jit(solution)/shard_map/all_to_all | solution.py:100
  681.0 0.5 fusion.66
  682.0 0.5 fusion.3
  682.6 0.5 fusion.21
  683.1 3.1 collective-permute-start
  686.2 3.0 collective-permute-done
  689.3 2.4 collective-permute-start.1
  691.7 5.2 collective-permute-done.1
  696.9 0.6 fusion.91
  (58 shorter events, 13.9 us)
Async XLA Ops:
  6.3 18.0 %copy-start.1 = (f32[128,128]{1,0:T(8,128)S(1)}, f32[128,128]{1,0:T(8,128)}, u32[]{:S(2)}) copy-start(f32[128,128]{1,0:T(8,128)} %param.8) | copy-start | bytes 196612
  6.3 30.3 %all-to-all-start = ((f32[2,1,1,128,128]{4,2,1,0,3:T(1,128)}), f32[2,1,1,128,128]{4,2,1,0,3:T(1,128)S(1)}, u32[]{:S(2)}, u32[]{:S(2)}) async-start(f32[2,1,1,128,128]{4,2,1,0,3:T(1,128)} %copy.11), calls=%async_computation | async-start | bytes 262144 | tf_op jit(solution)/shard_map/all_to_all | solution.py:100
  86.5 0.8 copy-start.3
  111.5 0.8 copy-start.4
  363.7 293.8 %copy-start = (f32[128,128]{1,0:T(8,128)}, f32[128,128]{1,0:T(8,128)S(1)}, u32[]{:S(2)}) copy-start(f32[128,128]{1,0:T(8,128)S(1)} %get-tuple-element.7) | copy-start | bytes 196612
  392.0 261.7 %all-to-all-start.5 = ((f32[2,1,128,1,128]{4,3,1,0,2:T(1,128)}), f32[2,1,128,1,128]{4,3,1,0,2:T(1,128)S(1)}, u32[]{:S(2)}, u32[]{:S(2)}) async-start(f32[2,1,128,1,128]{4,3,1,0,2:T(1,128)} %copy.22), calls=%async_computation.5 | async-start | bytes 262144 | tf_op jit(solution)/shard_map/all_to_all | solution.py:122
  683.1 6.2 collective-permute-start
  689.3 7.7 %copy-start.2 = (f32[128,32]{0,1:T(8,128)S(1)}, f32[128,32]{0,1:T(8,128)}, u32[]{:S(2)}) copy-start(f32[128,32]{0,1:T(8,128)} %param.9) | copy-start | bytes 49156
  689.3 7.7 %collective-permute-start.1 = (f32[128,128]{0,1:T(8,128)S(1)}, f32[128,128]{0,1:T(8,128)S(1)}, u32[]{:S(2)}, u32[]{:S(2)}) collective-permute-start(f32[128,128]{0,1:T(8,128)S(1)} %add.649), channel_id=1, source_target_pairs={{0,256},{128,384},{256,0},{384,128},{1,257},{129,385},{257,1},{385... | collective-permute-start | bytes 196616 | tf_op jit(solution)/shard_map/ppermute | solution.py:15
